TPU v7x, 32 devices: a whole 2x2x4 slice. The times are simulated.
32 devices in a mesh: group: 4 (over x, core), shard: 8 (over z, y).
Axes of the slice: x: 2, y: 2, z: 4, core: 2. Of those that a mesh axis runs over, the one named last changes fastest.
Arguments:
- step_index: int32 [1], replicated, may hold values from 0 to 1023
- hidden: bfloat16 [4, 8192, 4608], P('group', 'shard'), may hold values from -600 to 600
- upstream: bfloat16 [4, 8192, 2304], P('group', 'shard'), may hold values from -40 to 40
- numerator: float32 [4, 4608, 2304], P('group', 'shard'), may hold values from -6 to 6
- push_weight: float32 [4], P('group'), may hold values from 0.5 to 2
Outputs:
- numerator_next: float32 [4, 4608, 2304], P('group', 'shard')
- weight_next: float32 [4], P('group')
- params: bfloat16 [4, 4608, 2304], P('group', 'shard')
All inputs are finite; a program needn't handle non-finite values.
Results may differ from a plain program's by a relative error of at most 0.009.
Values may be sent and summed in bfloat16 or wider, within the bound.
A program may use at most 128 MiB of HBM per device.

v0:
```python
import functools

import jax
import jax.numpy as jnp
from jax import lax
from jax.experimental import pallas as pl
from jax.experimental.pallas import tpu as pltpu
from jax.sharding import PartitionSpec as P

learning_rate = 0.3
decay_steps = 256.0
clip_ceiling = 1.0
epsilon = 1e-06
LANES = 128
LINKED = jnp.bfloat16
MESH = pl.DeviceIdType.MESH
FAR_FIRST_TILES = 3
NEAR_FIRST_TILES = (4, 4, 3, 2, 1, 1)
EARLY = 2


def wide(x):
    return x.astype(jnp.float32)


def cuts(width):
    tiles = width // LANES
    sizes = (FAR_FIRST_TILES,) + NEAR_FIRST_TILES
    if tiles != sum(sizes) or width % LANES:
        sizes = (LANES, LANES, width - 2 * LANES)
    else:
        sizes = tuple(s * LANES for s in sizes)
    starts = [sum(sizes[:i]) for i in range(len(sizes))]
    return list(zip(starts, sizes))


def step_of_rows(rows):
    for step in (64, 48, 32, 16):
        if rows % step == 0:
            return step
    return rows


def kernel(plan, partial, hidden, upstream, state, weight, grad, totals, *refs):
    groups, far, near, rows, pieces, offsets = (
        plan["groups"], plan["far"], plan["near"], plan["rows"], plan["pieces"], plan["offsets"]
    )
    levels, count, early = len(offsets), far * near, plan["early"]
    peer_states, peer_grads = refs[:levels], refs[levels : 2 * levels]
    refs = list(refs[2 * levels :])
    mine = [refs.pop(0) for _ in pieces]
    came = [None] + [refs.pop(0) for _ in pieces[1:]]
    slots = [refs.pop(0) for _ in pieces]
    turn_own, turn_out, turn_in, norms, own_total, units, cotangent = (refs.pop(0) for _ in range(7))
    (load_sem, fetch_sem, near_send, near_recv, up_send, up_recv, down_send, down_recv, turn_sem, state_send, state_recv,
     grad_send, grad_recv, norm_send, norm_recv, total_send, total_recv) = refs

    g, s = lax.axis_index("group"), lax.axis_index("shard")
    z, y = s // near, s % near
    near_peer = (g, z * near + (near - 1 - y))
    above = (g, (s + near) % count)
    below = (g, (s + count - near) % count)
    step_rows = step_of_rows(rows)

    barrier = pltpu.get_barrier_semaphore()
    for d in range(1, count):
        pl.semaphore_signal(barrier, inc=1, device_id=(g, (s + d) % count), device_id_type=MESH)
    for d in range(1, groups):
        pl.semaphore_signal(barrier, inc=1, device_id=((g + d) % groups, s), device_id_type=MESH)
    pl.semaphore_wait(barrier, count - 1 + groups - 1)

    def remote(src, dst, send, recv, device):
        return pltpu.make_async_remote_copy(
            src_ref=src, dst_ref=dst, send_sem=send, recv_sem=recv, device_id=device, device_id_type=MESH
        )

    def near_copy(c):
        start, size = pieces[c]
        source = partial.at[:, near - 1 - y, :, pl.ds(start, size)] if c < early else mine[c].at[:, near - 1 - y]
        return remote(source, came[c], near_send.at[c], near_recv.at[c], near_peer)

    def load_copy(c):
        start, size = pieces[c]
        at = partial.at[:, :, :, pl.ds(start, size)] if c == 0 else partial.at[:, y, :, pl.ds(start, size)]
        return pltpu.make_async_copy(at, mine[c], load_sem.at[c])

    def up_copy(c, t, b):
        return remote(slots[c].at[b], slots[c].at[b], up_send.at[c, t], up_recv.at[c, t], above)

    def down_copy(c, t, b):
        to = far if t == far - 2 else b
        return remote(slots[c].at[b], slots[c].at[to], down_send.at[c, t], down_recv.at[c, t], below)

    def state_copy(l):
        return remote(
            state, peer_states[l], state_send.at[l], state_recv.at[l], ((g + offsets[l]) % groups, s)
        )

    def grad_copy(c, l):
        start, size = pieces[c]
        return remote(
            grad.at[:, pl.ds(start, size)],
            peer_grads[l].at[:, pl.ds(start, size)],
            grad_send.at[c, l],
            grad_recv.at[c, l],
            ((g + offsets[l]) % groups, s),
        )

    def each_rows(body):
        def once(i, carry):
            body(pl.ds(pl.multiple_of(i * step_rows, step_rows), step_rows))
            return carry

        lax.fori_loop(0, rows // step_rows, once, 0)

    def term(c, b, r, half):
        if c == 0:
            return wide(mine[0][b, half, r, :])
        own = mine[c][b, r, :] if c < early else mine[c][b, y, r, :]
        return wide(own) + wide(came[c][b, r, :])

    def compute(c):
        start, size = pieces[c]
        tile = plan["tile"]
        blocks = tile // (near * rows)
        skipped = pieces[early][0]

        def once(k, carry):
            product = lax.dot_general(
                units[:, pl.ds(pl.multiple_of(k * tile, tile), tile)],
                cotangent[:, pl.ds(start - skipped, size)],
                (((0,), (0,)), ((), ())),
                preferred_element_type=jnp.float32,
            )
            mine[c][pl.ds(k * blocks, blocks)] = product.astype(LINKED).reshape(blocks, near, rows, size)
            return carry

        lax.fori_loop(0, far * near * rows // tile, once, 0)

    def slot(c, b, r, half):
        return slots[c][b, half, r, :] if c == 0 else slots[c][b, r, :]

    def store_slot(c, b, r, half, value):
        if c == 0:
            slots[c][b, half, r, :] = value.astype(LINKED)
        else:
            slots[c][b, r, :] = value.astype(LINKED)

    def halves(c):
        return range(near) if c == 0 else range(1)

    def fill(c, b, add):
        for half in halves(c):
            def body(r):
                value = term(c, b, r, half)
                if add:
                    value = value + wide(slot(c, b, r, half))
                store_slot(c, b, r, half, value)

            each_rows(body)

    def line_step(c, t):
        up_b = far - 1 - t + z
        down_b = t - (far - 1) + z

        @pl.when(z == 0)
        def _():
            fill(c, up_b, False)
            up_copy(c, t, up_b).start()

        if t > 0:
            @pl.when((z > 0) & (z <= t) & (z < far - 1))
            def _():
                up_copy(c, t - 1, up_b).wait_recv()
                fill(c, up_b, True)
                up_copy(c, t, up_b).start()

        @pl.when(z == far - 1)
        def _():
            fill(c, down_b, False)
            down_copy(c, t, down_b).start()

        if t > 0:
            @pl.when((z < far - 1) & (z >= far - 1 - t) & (z > 0))
            def _():
                down_copy(c, t - 1, down_b).wait_recv()
                fill(c, down_b, True)
                down_copy(c, t, down_b).start()

    def own_value(c, r, half):
        value = term(c, z, r, half)
        below_term = jnp.where(z > 0, wide(slot(c, z, r, half)), 0.0)
        above_term = jnp.where(z < far - 1, wide(slot(c, far, r, half)), 0.0)
        return value + below_term + above_term

    def wait_own(c):
        @pl.when(z > 0)
        def _():
            up_copy(c, far - 2, z).wait_recv()

        @pl.when(z < far - 1)
        def _():
            down_copy(c, far - 2, far).wait_recv()

    def settle(c, r, value):
        start, size = pieces[c]
        grad[r, pl.ds(start, size)] = value.astype(LINKED)
        square = value * value
        total = jnp.zeros((8, LANES), jnp.float32)
        for i in range(0, step_rows, 8):
            for j in range(0, size, LANES):
                total = total + square[i : i + 8, j : j + LANES]
        own_total[0] = own_total[0] + total

    def finish(c):
        wait_own(c)
        if c == 0:
            def put(r):
                turn_own[r, :] = own_value(0, r, y)
                turn_out[r, :] = own_value(0, r, near - 1 - y).astype(LINKED)

            each_rows(put)
            remote(turn_out, turn_in, turn_sem.at[0], turn_sem.at[1], near_peer).start()
            return
        each_rows(lambda r: settle(c, r, own_value(c, r, 0)))
        for l in range(levels):
            grad_copy(c, l).start()

    def finish_turn():
        remote(turn_out, turn_in, turn_sem.at[0], turn_sem.at[1], near_peer).wait()
        each_rows(lambda r: settle(0, r, turn_own[r, :] + wide(turn_in[r, :])))
        for l in range(levels):
            grad_copy(0, l).start()

    last = len(pieces) - 1
    skipped = pieces[early][0] if early <= last else 0
    fetch_units = pltpu.make_async_copy(hidden, units, fetch_sem.at[0])
    fetch_cotangent = pltpu.make_async_copy(
        upstream.at[:, pl.ds(skipped, upstream.shape[1] - skipped)], cotangent, fetch_sem.at[1]
    )
    load_copy(0).start()
    for c in range(1, early):
        near_copy(c).start()
    fetch_units.start()
    fetch_cotangent.start()
    for l in range(levels):
        state_copy(l).start()
    for c in range(1, early):
        load_copy(c).start()
    own_total[0] = jnp.zeros((8, LANES), jnp.float32)
    own_total[1] = weight[...]

    load_copy(0).wait()
    later = list(range(early, last + 1))
    for t in range(far - 1):
        line_step(0, t)
        if t == 0:
            fetch_units.wait()
            fetch_cotangent.wait()
        if later:
            c = later.pop(0)
            compute(c)
            if c == early:
                near_copy(c).start()
    for c in later:
        compute(c)
    for c in range(1, last + 1):
        near_copy(c).wait()
        if c + 2 <= last:
            near_copy(c + 2).start()
        if c < early:
            load_copy(c).wait()
        line_step(c, 0)
        finish(c - 1)
        if c == 3 or (c == last and last < 3):
            finish_turn()
        for t in range(1, far - 1):
            line_step(c, t)
    finish(last)

    norms[s] = own_total[0]
    for d in range(1, count):
        remote(norms.at[s], norms.at[s], norm_send.at[d], norm_recv.at[d], (g, (s + d) % count)).start()
    for d in range(1, count):
        remote(norms.at[s], norms.at[(s + count - d) % count], norm_send.at[d], norm_recv.at[d], (g, (s + d) % count)).wait_recv()
    total = norms[0]
    for d in range(1, count):
        total = total + norms[d]
    own_total[0] = total
    totals[0] = own_total[...]

    def total_copy(l):
        return remote(
            own_total, totals.at[l + 1], total_send.at[l], total_recv.at[l], ((g + offsets[l]) % groups, s)
        )

    for l in range(levels):
        total_copy(l).start()
    for d in range(1, count):
        remote(norms.at[s], norms.at[s], norm_send.at[d], norm_recv.at[d], (g, (s + d) % count)).wait_send()
    for c in range(last + 1):
        for t in range(far - 1):
            @pl.when((z <= t) & (z < far - 1))
            def _():
                up_copy(c, t, far - 1 - t + z).wait_send()

            @pl.when((z >= far - 1 - t) & (z > 0))
            def _():
                down_copy(c, t, t - (far - 1) + z).wait_send()

        for l in range(levels):
            grad_copy(c, l).wait()
    for l in range(levels):
        state_copy(l).wait()
        total_copy(l).wait()


def reduced(partial, hidden, upstream, state, weight, plan):
    far, near, rows, pieces = plan["far"], plan["near"], plan["rows"], plan["pieces"]
    levels, count, width = len(plan["offsets"]), far * near, state.shape[1]
    anywhere, vmem = pl.BlockSpec(memory_space=pl.ANY), pl.BlockSpec(memory_space=pltpu.VMEM)
    first = pieces[0][1]
    scratch = [pltpu.VMEM((far, near, rows, first), LINKED)]
    early = plan["early"]
    scratch += [pltpu.VMEM((far, rows, size), LINKED) for _, size in pieces[1:early]]
    scratch += [pltpu.VMEM((far, near, rows, size), LINKED) for _, size in pieces[early:]]
    scratch += [pltpu.VMEM((far, rows, size), LINKED) for _, size in pieces[1:]]
    scratch += [pltpu.VMEM((far + 1, near, rows, first), LINKED)]
    scratch += [pltpu.VMEM((far + 1, rows, size), LINKED) for _, size in pieces[1:]]
    scratch += [pltpu.VMEM((rows, first), jnp.float32)] + [pltpu.VMEM((rows, first), LINKED)] * 2
    scratch += [pltpu.VMEM((count, 8, LANES), jnp.float32), pltpu.VMEM((2, 8, LANES), jnp.float32)]
    scratch += [pltpu.VMEM(hidden.shape, LINKED), pltpu.VMEM((hidden.shape[0], width - pieces[early][0]), LINKED)]
    n = len(pieces)
    dma = pltpu.SemaphoreType.DMA
    scratch += [dma((n,)), dma((2,))] + [dma((n,))] * 2 + [dma((n, far - 1))] * 4 + [dma((2,))] + [dma((levels,))] * 2
    scratch += [dma((n, levels))] * 2 + [dma((count,))] * 2 + [dma((levels,))] * 2
    linked = jax.ShapeDtypeStruct((rows, width), LINKED)
    return pl.pallas_call(
        functools.partial(kernel, plan),
        out_shape=[
            linked,
            jax.ShapeDtypeStruct((levels + 1, 2, 8, LANES), jnp.float32),
        ]
        + [linked] * (2 * levels),
        in_specs=[anywhere] * 4 + [vmem],
        out_specs=[vmem, vmem] + [anywhere] * (2 * levels),
        scratch_shapes=scratch,
        compiler_params=pltpu.CompilerParams(
            collective_id=0, has_side_effects=True, vmem_limit_bytes=63 * 1024 * 1024
        ),
    )(partial, hidden, upstream, state, weight)


def shards(step_index, hidden, upstream, numerator, push_weight):
    own_state = numerator[0]
    groups = lax.axis_size("group")
    count = lax.axis_size("shard")
    near = 2
    level_count = groups.bit_length() - 1
    offset_bit = step_index[0] % level_count
    rate = learning_rate / jnp.sqrt(1.0 + step_index[0].astype(jnp.float32) / decay_steps)
    rows, width = own_state.shape
    entry_count = rows * count * width
    plan = {
        "groups": groups,
        "far": count // near,
        "near": near,
        "rows": rows,
        "pieces": cuts(width),
        "early": EARLY,
        "tile": next(t for t in (1152, rows * count) if rows * count % t == 0 and t % (near * rows) == 0),
        "offsets": tuple(1 << bit for bit in range(level_count)),
    }
    columns = plan["pieces"][EARLY][0]
    partial = lax.dot_general(
        hidden[0], upstream[0][:, :columns], (((0,), (0,)), ((), ())), preferred_element_type=jnp.float32
    ).astype(LINKED)
    weight = jnp.broadcast_to(push_weight[0], (8, LANES))
    gradient, totals, *peers = reduced(
        partial.reshape(count // near, near, rows, columns),
        hidden[0],
        upstream[0],
        own_state.astype(LINKED),
        weight,
        plan,
    )
    gradient = wide(gradient)
    squares = jnp.sum(totals[:, 0], axis=(1, 2))
    factors = rate * jnp.minimum(1.0, clip_ceiling / jnp.sqrt(squares / entry_count + epsilon))

    def chosen(values):
        got = values[0]
        for bit in range(1, level_count):
            got = jnp.where(offset_bit == bit, values[bit], got)
        return got

    peer_state = wide(chosen(peers[:level_count]))
    peer_gradient = wide(chosen(peers[level_count:]))
    peer_factor = chosen([factors[bit + 1] for bit in range(level_count)])
    peer_weight = chosen([totals[bit + 1, 1, 0, 0] for bit in range(level_count)])
    mixed_state = 0.5 * (own_state - factors[0] * gradient + (peer_state - peer_factor * peer_gradient))
    weight_next = 0.5 * (push_weight + peer_weight)
    new_params = (mixed_state / weight_next[0]).astype(jnp.bfloat16)
    return (mixed_state[None], weight_next, new_params[None])


def solution(mesh):
    placed = (
        P(),
        P("group", "shard", None),
        P("group", "shard", None),
        P("group", "shard", None),
        P("group"),
    )
    return jax.shard_map(
        shards,
        mesh=mesh,
        in_specs=placed,
        out_specs=(P("group", "shard", None), P("group"), P("group", "shard", None)),
        check_vma=False,
    )
```

profile of v0, /device:TPU:0, one launch (start us, length us, event | category | flops | bytes accessed | tf_op | source)
XLA Modules:
  0.0 273.5 jit_solution(6881098103137384571)
XLA Ops:
  2.0 0.6 broadcast_in_dim.9.weight
  2.6 4.3 %bitcast_convert_fusion.state = bf16[576,2304]{1,0:T(8,128)(2,1)} fusion(f32[1,576,2304]{2,1,0:T(8,128)} %param.8), kind=kLoop, calls=%fused_computation.2 | loop fusion | flops 1327104 | bytes 7962624 | tf_op jit(solution)/shard_map/convert_element_type | solution.py:383
  6.8 15.1 %convolution_convert_fusion = bf16[4608,896]{1,0:T(8,128)(2,1)} fusion(bf16[1024,2304]{1,0:T(8,128)(2,1)} %bitcast.33, bf16[1,1024,4608]{2,1,0:T(8,128)(2,1)} %param.6), kind=kOutput, calls=%fused_computation | convolution fusion | flops 8459845632 | bytes 19529728 | tf_op jit(solution)/shard_map/dot_general | solution.py:375
  22.0 236.5 %shard_map.76 = (bf16[576,2304]{1,0:T(8,128)(2,1)}, f32[3,2,8,128]{3,2,1,0:T(8,128)}, bf16[576,2304]{1,0:T(8,128)(2,1)}, bf16[576,2304]{1,0:T(8,128)(2,1)}, bf16...) custom-call(bf16[4,2,576,896]{3,2,1,0:T(8,128)(2,1)} %bitcast.31, bf16[1024,4608]{1,0:T(8,128)(2,1)} %bitcast.30, ...), custom_call_target="tpu_custom_call" | custom-call | tf_op jit(solution)/shard_map/pallas_call | solution.py:338
  258.4 0.8 slice_reduce_fusion
  259.2 1.2 fusion.6
  261.8 0.6 fusion.7
  263.6 8.7 %fusion.2 = (bf16[1,576,2304]{2,1,0:T(8,128)(2,1)}, f32[576,2304]{1,0:T(8,128)}) fusion(f32[]{:T(128)} %bitcast.13, bf16[576,2304]{1,0:T(8,128)(2,1)} %get-tuple-element.13, bf16[576,2304]{1,0:T(8,128)(2,1)} %get-tuple-element.14, f32[]{:T(128)S(6)} %select_n.29, bf16[576,2304]{1,0:T(8,128)(2,1)} %get-tuple-element.11, ...), kind=kLoop, calls=%fused_computation.6 | loop fusion | flops 17252352 | bytes 26542092 | tf_op jit(solution)/shard_map/broadcast_in_dim | solution.py:404
  (1 shorter events, 0.0 us)
where the time goes:
time: 274 us; the launch traced here: 273 us
  Pallas kernels  236 us (86%)
  matrix products  15.1 us (6%)
  other arithmetic  13.8 us (5%)
  between operations  5.73 us (2%)
    pallas_call x1, Pallas kernels, reduced(): pl.pallas_call(functools.partial(kernel, plan), out_shape=[linked, jax.Sh...  236 us
    dot_general x1, matrix products, shards(): lax.dot_general(hidden[0], upstream[0][:, :columns], (((0,), (0,)), ((),...  15.1 us
    broadcast_in_dim x1, other arithmetic, shards(): return (mixed_state[None], weight_next, new_params[None])  8.7 us

commit v1 on v0

v1 whole, which is shorter than its diff:
```python
import functools

import jax
import jax.numpy as jnp
from jax import lax
from jax.experimental import pallas as pl
from jax.experimental.pallas import tpu as pltpu
from jax.sharding import PartitionSpec as P

learning_rate = 0.3
decay_steps = 256.0
clip_ceiling = 1.0
epsilon = 1e-06
LANES = 128
LINKED = jnp.bfloat16
MESH = pl.DeviceIdType.MESH
NEAR = 2
AHEAD = 3
RING = 4
FLIGHT = 2


def wide(x):
    return x.astype(jnp.float32)


def step_of_rows(rows):
    for step in (96, 64, 48, 32, 16):
        if rows % step == 0:
            return step
    return rows


def kernel(plan, hidden, upstream, state, weight, grad, totals, peer_states, peer_grads, *refs):
    groups, far, near, rows, offsets = (plan[k] for k in ("groups", "far", "near", "rows", "offsets"))
    first, pieces, splits, tile = (plan[k] for k in ("first", "pieces", "splits", "tile"))
    levels, count, half = len(offsets), far * near, rows // splits
    (units, cotangent, own, away, came, slots, first_own, first_slots, turn_own, turn_out, turn_in, cast, stage,
     running, norms, fetch_sem, stage_sem, near_send, near_recv, up_send, up_recv, down_send, down_recv,
     first_up_send, first_up_recv, first_down_send, first_down_recv, turn_send, turn_recv, state_send, state_recv,
     grad_send, grad_recv, norm_send, norm_recv) = refs

    g, s = lax.axis_index("group"), lax.axis_index("shard")
    z, y = s // near, s % near
    near_peer = (g, z * near + (near - 1 - y))
    above = (g, (s + near) % count)
    below = (g, (s + count - near) % count)
    chunks, blocks = far * near * rows // tile, tile // (near * rows)
    chunk_rows = stage.shape[1]

    receivers = [(0, d) for d in range(1, count)]
    receivers += [(d, e) for d in range(1, groups) for e in range(count)]
    barrier = pltpu.get_barrier_semaphore()
    for d, e in receivers:
        pl.semaphore_signal(barrier, inc=1, device_id=((g + d) % groups, (s + e) % count), device_id_type=MESH)

    def remote(src, dst, send, recv, device):
        return pltpu.make_async_remote_copy(
            src_ref=src, dst_ref=dst, send_sem=send, recv_sem=recv, device_id=device, device_id_type=MESH
        )

    def part(h):
        return pl.ds(h * half, half)

    def columns(at, size=LANES):
        return pl.ds(pl.multiple_of(at * LANES, LANES), size)

    def near_copy(c, h):
        return remote(
            away.at[c % RING, :, part(h)], came.at[c, :, part(h)], near_send.at[c, h], near_recv.at[c, h], near_peer
        )

    def up_copy(c, h, t, b):
        at = slots.at[c, b, part(h)]
        return remote(at, at, up_send.at[c, h, t], up_recv.at[c, h, t], above)

    def down_copy(c, h, t, b):
        to = jnp.where(t == far - 2, far, b)
        return remote(
            slots.at[c, b, part(h)], slots.at[c, to, part(h)], down_send.at[c, h, t], down_recv.at[c, h, t], below
        )

    def first_up_copy(j, t, b):
        at = first_slots.at[j, b]
        return remote(at, at, first_up_send.at[j, t], first_up_recv.at[j, t], above)

    def first_down_copy(j, t, b):
        to = jnp.where(t == far - 2, far, b)
        return remote(
            first_slots.at[j, b], first_slots.at[j, to], first_down_send.at[j, t], first_down_recv.at[j, t], below
        )

    def turn_copy(j):
        return remote(turn_out.at[j], turn_in.at[j], turn_send.at[j], turn_recv.at[j], near_peer)

    def state_copy(l):
        return remote(cast, peer_states.at[l], state_send.at[l], state_recv.at[l], ((g + offsets[l]) % groups, s))

    def grad_copy(at, h, l):
        return remote(
            grad.at[part(h), columns(at)],
            peer_grads.at[l, part(h), columns(at)],
            grad_send.at[at, h, l],
            grad_recv.at[at, h, l],
            ((g + offsets[l]) % groups, s),
        )

    def each_rows(body):
        step = step_of_rows(rows)

        def once(i, carry):
            body(pl.ds(pl.multiple_of(i * step, step), step))
            return carry

        lax.fori_loop(0, rows // step, once, 0)

    def loop(low, high, body):
        def once(i, carry):
            body(i)
            return carry

        lax.fori_loop(low, high, once, 0)

    def fetch_units(k):
        at = pl.ds(pl.multiple_of(k * tile, tile), tile)
        return pltpu.make_async_copy(hidden.at[:, at], units.at[:, at], fetch_sem.at[k])

    def fetch_cotangent(i, low, high):
        at = pl.ds(low * LANES, (high - low) * LANES)
        return pltpu.make_async_copy(upstream.at[:, at], cotangent.at[:, at], fetch_sem.at[chunks + i])

    def compute(at, places, loading=False):
        size = len(places) * LANES

        def once(k):
            if loading:
                fetch_units(k).wait()
            product = lax.dot_general(
                units[:, pl.ds(pl.multiple_of(k * tile, tile), tile)],
                cotangent[:, columns(at, size)],
                (((0,), (0,)), ((), ())),
                preferred_element_type=jnp.float32,
            ).reshape(blocks, near, rows, size)
            to = pl.ds(k * blocks, blocks)
            for i, (kind, index) in enumerate(places):
                piece = product[:, :, :, i * LANES : (i + 1) * LANES]
                if kind == "first":
                    first_own[index, to] = piece.astype(LINKED)
                else:
                    own[index, to] = jnp.where(y == 0, piece[:, 0], piece[:, 1]).astype(LINKED)
                    away[index % RING, to] = jnp.where(y == 0, piece[:, 1], piece[:, 0]).astype(LINKED)

        loop(0, chunks, once)

    def line(t, edge, middle, fill, up, down):
        up_b = far - 1 - t + z
        down_b = t - (far - 1) + z
        if edge:
            @pl.when(z == 0)
            def _():
                fill(up_b, False)
                up(t, up_b).start()

            @pl.when(z == far - 1)
            def _():
                fill(down_b, False)
                down(t, down_b).start()

        if middle:
            @pl.when((z > 0) & (z <= t) & (z < far - 1))
            def _():
                up(t - 1, up_b).wait_recv()
                fill(up_b, True)
                up(t, up_b).start()

            @pl.when((z < far - 1) & (z >= far - 1 - t) & (z > 0))
            def _():
                down(t - 1, down_b).wait_recv()
                fill(down_b, True)
                down(t, down_b).start()

    def term(c, h, b):
        return wide(own[c, b, part(h), :]) + wide(came[c, b, part(h), :])

    def line_step(c, h, t):
        def fill(b, add):
            value = term(c, h, b)
            if add:
                value = value + wide(slots[c, b, part(h), :])
            slots[c, b, part(h), :] = value.astype(LINKED)

        line(t, True, True, fill, lambda t, b: up_copy(c, h, t, b), lambda t, b: down_copy(c, h, t, b))

    def first_step(j, t, edge, middle):
        def fill(b, add):
            for side in range(near):
                def body(r):
                    value = first_own[j, b, side, r, :]
                    if add:
                        value = (wide(value) + wide(first_slots[j, b, side, r, :])).astype(LINKED)
                    first_slots[j, b, side, r, :] = value

                each_rows(body)

        line(t, edge, middle, fill, lambda t, b: first_up_copy(j, t, b), lambda t, b: first_down_copy(j, t, b))

    def settle(at, h, value):
        grad[part(h), columns(at)] = value.astype(LINKED)
        square = value * value
        total = square[0:8]
        for i in range(8, half, 8):
            total = total + square[i : i + 8]
        running[0] = running[0] + total
        for l in range(levels):
            grad_copy(at, h, l).start()

    def wait_own(up, down):
        @pl.when(z > 0)
        def _():
            up(far - 2, z).wait_recv()

        @pl.when(z < far - 1)
        def _():
            down(far - 2, far).wait_recv()

    def finish(c, h):
        wait_own(lambda t, b: up_copy(c, h, t, b), lambda t, b: down_copy(c, h, t, b))
        value = term(c, h, z)
        value = value + jnp.where(z > 0, wide(slots[c, z, part(h), :]), 0.0)
        value = value + jnp.where(z < far - 1, wide(slots[c, far, part(h), :]), 0.0)
        settle(first + c, h, value)

    def finish_first(j):
        wait_own(lambda t, b: first_up_copy(j, t, b), lambda t, b: first_down_copy(j, t, b))

        def put(r):
            def own_value(side):
                value = wide(first_own[j, z, side, r, :])
                value = value + jnp.where(z > 0, wide(first_slots[j, z, side, r, :]), 0.0)
                return value + jnp.where(z < far - 1, wide(first_slots[j, far, side, r, :]), 0.0)

            turn_own[j, r, :] = own_value(y)
            turn_out[j, r, :] = own_value(near - 1 - y).astype(LINKED)

        each_rows(put)
        turn_copy(j).start()

    def finish_turn(j):
        turn_copy(j).wait()
        for h in range(splits):
            settle(first - 1 - j, h, turn_own[j, part(h), :] + wide(turn_in[j, part(h), :]))

    steps = first * (far - 1)
    span = max(1, pieces - 3)

    def reached(c):
        goal = far - 1 + lax.div((c + 1) * (steps - (far - 1)), span)
        return jnp.where(c < 0, 0, jnp.minimum(steps, goal))

    def when(condition, body):
        pl.when(condition)(body)

    lead = (first - 1, first + 1)
    fetch_cotangent(0, *lead).start()
    loop(0, chunks, lambda k: fetch_units(k).start())
    fetch_cotangent(1, lead[1], first + pieces).start()
    fetch_cotangent(2, 0, lead[0]).start()
    running[0] = jnp.zeros((8, LANES), jnp.float32)
    running[1] = weight[...]
    fetch_cotangent(0, *lead).wait()
    compute(first - 1, [("first", 0), ("near", 0)], loading=True)
    pl.semaphore_wait(barrier, len(receivers))
    for k in range(FLIGHT):
        near_copy(k // splits, k % splits).start()
    loop(0, far - 1, lambda t: first_step(0, t, True, False))
    fetch_cotangent(1, lead[1], first + pieces).wait()
    fetch_cotangent(2, 0, lead[0]).wait()
    compute(first + 1, [("near", c) for c in range(1, AHEAD)])
    compute(0, [("first", j) for j in range(first - 1, 0, -1)])

    def stage_copy(i):
        return pltpu.make_async_copy(
            state.at[pl.ds(pl.multiple_of(i * chunk_rows, chunk_rows), chunk_rows)], stage.at[i % 2], stage_sem.at[i % 2]
        )

    stage_copy(0).start()

    def cast_rows(i):
        stage_copy(i).wait()
        when(i + 1 < rows // chunk_rows, lambda: stage_copy(i + 1).start())
        cast[pl.ds(pl.multiple_of(i * chunk_rows, chunk_rows), chunk_rows), :] = stage[i % 2].astype(LINKED)

    loop(0, rows // chunk_rows, cast_rows)
    for l in range(levels):
        state_copy(l).start()

    def prepare(c):
        for h in range(splits):
            when(c >= RING, lambda: near_copy(c - RING, h).wait_send())
        compute(first + c, [("near", c)])

    def tick(c):
        for h in range(splits):
            done = c - (far - 1)
            when((done >= 0) & (done < pieces), lambda: finish(done, h))

            def older(i):
                t = far - 2 - i
                when((c - t >= 0) & (c - t < pieces), lambda: line_step(c - t, h, t))

            loop(0, far - 2, older)

            @pl.when(c < pieces)
            def _():
                near_copy(c, h).wait_recv()
                later = c + (h + FLIGHT) // splits
                when(later < pieces, lambda: near_copy(later, (h + FLIGHT) % splits).start())
                line_step(c, h, 0)

            if h == 0:
                when(c + AHEAD < pieces, lambda: prepare(c + AHEAD))
        loop(lax.div(reached(c - 3), far - 1), lax.div(reached(c - 2), far - 1), finish_turn)
        loop(lax.div(reached(c - 2), far - 1), lax.div(reached(c - 1), far - 1), finish_first)

        def first_at(q):
            j, t = lax.div(q, far - 1), lax.rem(q, far - 1)
            when(j > 0, lambda: first_step(j, t, True, False))
            first_step(j, t, False, True)

        loop(reached(c - 1), reached(c), first_at)

    loop(0, pieces + far - 1, tick)

    def norm_copy(l, s_from, e):
        d = 0 if l == 0 else offsets[l - 1]
        at = norms.at[l, s_from]
        return remote(running, at, norm_send.at[l, e], norm_recv.at[l, e], ((g + d) % groups, (s + e) % count))

    messages = [(l, e) for l in range(levels + 1) for e in range(count) if l or e]
    for l, e in messages:
        norm_copy(l, s, e).start()
    norms[0, s] = running[...]
    for l, e in messages:
        norm_copy(l, (s + count - e) % count, e).wait_recv()
    for l in range(levels + 1):
        total = norms[l, 0, 0]
        for d in range(1, count):
            total = total + norms[l, d, 0]
        totals[l, 0] = total
        totals[l, 1] = norms[l, 0, 1]

    for l, e in messages:
        norm_copy(l, s, e).wait_send()

    def drain_line(t, up, down):
        @pl.when((z <= t) & (z < far - 1))
        def _():
            up(t, far - 1 - t + z).wait_send()

        @pl.when((z >= far - 1 - t) & (z > 0))
        def _():
            down(t, t - (far - 1) + z).wait_send()

    def drain(c):
        for h in range(splits):
            when(c >= pieces - RING, lambda: near_copy(c, h).wait_send())
            loop(0, far - 1, lambda t: drain_line(
                t, lambda t, b: up_copy(c, h, t, b), lambda t, b: down_copy(c, h, t, b)))

    def drain_first(j):
        loop(0, far - 1, lambda t: drain_line(
            t, lambda t, b: first_up_copy(j, t, b), lambda t, b: first_down_copy(j, t, b)))

    def drain_grads(at):
        for h in range(splits):
            for l in range(levels):
                grad_copy(at, h, l).wait()

    loop(0, pieces, drain)
    loop(0, first, drain_first)
    loop(0, first + pieces, drain_grads)
    for l in range(levels):
        state_copy(l).wait()


def reduced(hidden, upstream, state, weight, plan):
    far, near, rows, first, pieces, splits = (plan[k] for k in ("far", "near", "rows", "first", "pieces", "splits"))
    levels, count, width = len(plan["offsets"]), far * near, state.shape[1]
    anywhere, vmem = pl.BlockSpec(memory_space=pl.ANY), pl.BlockSpec(memory_space=pltpu.VMEM)
    dma, single = pltpu.SemaphoreType.DMA, jnp.float32
    scratch = [
        pltpu.VMEM(hidden.shape, LINKED),
        pltpu.VMEM(upstream.shape, LINKED),
        pltpu.VMEM((pieces, far, rows, LANES), LINKED),
        pltpu.VMEM((RING, far, rows, LANES), LINKED),
        pltpu.VMEM((pieces, far, rows, LANES), LINKED),
        pltpu.VMEM((pieces, far + 1, rows, LANES), LINKED),
        pltpu.VMEM((first, far, near, rows, LANES), LINKED),
        pltpu.VMEM((first, far + 1, near, rows, LANES), LINKED),
        pltpu.VMEM((first, rows, LANES), single),
        pltpu.VMEM((first, rows, LANES), LINKED),
        pltpu.VMEM((first, rows, LANES), LINKED),
        pltpu.VMEM((rows, width), LINKED),
        pltpu.VMEM((2, step_of_rows(rows), width), single),
        pltpu.VMEM((2, 8, LANES), single),
        pltpu.VMEM((levels + 1, count, 2, 8, LANES), single),
        dma((far * near * rows // plan["tile"] + 3,)),
        dma((2,)),
    ]
    scratch += [dma((pieces, splits))] * 2 + [dma((pieces, splits, far - 1))] * 4 + [dma((first, far - 1))] * 4
    scratch += [dma((first,))] * 2 + [dma((levels,))] * 2 + [dma((first + pieces, splits, levels))] * 2
    scratch += [dma((levels + 1, count))] * 2
    peers = jax.ShapeDtypeStruct((levels, rows, width), LINKED)
    return pl.pallas_call(
        functools.partial(kernel, plan),
        out_shape=[
            jax.ShapeDtypeStruct((rows, width), LINKED),
            jax.ShapeDtypeStruct((levels + 1, 2, 8, LANES), single),
            peers,
            peers,
        ],
        in_specs=[anywhere] * 3 + [vmem],
        out_specs=[vmem, vmem, anywhere, anywhere],
        scratch_shapes=scratch,
        compiler_params=pltpu.CompilerParams(
            collective_id=0, has_side_effects=True, vmem_limit_bytes=63 * 1024 * 1024
        ),
    )(hidden, upstream, state, weight)


def update(levels, entry_count, step, totals, state, grad, peer_state, peer_grad, mixed_out, params_out, weight_out):
    bit = lax.rem(step[0], levels)
    rate = learning_rate / jnp.sqrt(1.0 + jnp.full((8, LANES), step[0], jnp.int32).astype(jnp.float32) / decay_steps)

    def factor(l):
        squares = jnp.sum(totals[l, 0], keepdims=True)
        return (rate * jnp.minimum(1.0, clip_ceiling / jnp.sqrt(squares / entry_count + epsilon)))[0:1, 0:1]

    mine, other = factor(0), factor(1 + bit)
    weight_next = 0.5 * (totals[0, 1] + totals[1 + bit, 1])
    weight_out[0] = jnp.max(weight_next)
    pushed = state[...] - mine * wide(grad[...])
    came = wide(peer_state[0]) - other * wide(peer_grad[0])
    mixed = 0.5 * (pushed + came)
    mixed_out[...] = mixed
    params_out[...] = (mixed * (1.0 / weight_next)[0:1, 0:1]).astype(jnp.bfloat16)


def updated(step_index, totals, state, grad, peer_states, peer_grads, entry_count):
    levels, (rows, width) = peer_states.shape[0], state.shape
    step = step_of_rows(rows)
    here = pl.BlockSpec((step, width), lambda i, at: (i, 0))
    chosen = pl.BlockSpec((1, step, width), lambda i, at: (lax.rem(at[0], levels), i, 0))
    return pl.pallas_call(
        functools.partial(update, levels, entry_count),
        out_shape=[
            jax.ShapeDtypeStruct((rows, width), jnp.float32),
            jax.ShapeDtypeStruct((rows, width), jnp.bfloat16),
            jax.ShapeDtypeStruct((1,), jnp.float32),
        ],
        grid_spec=pltpu.PrefetchScalarGridSpec(
            num_scalar_prefetch=1,
            grid=(rows // step,),
            in_specs=[pl.BlockSpec(totals.shape, lambda i, at: (0, 0, 0, 0)), here, here, chosen, chosen],
            out_specs=[here, here, pl.BlockSpec(memory_space=pltpu.SMEM)],
        ),
    )(step_index, totals, state, grad, peer_states, peer_grads)


def shards(step_index, hidden, upstream, numerator, push_weight):
    own_state = numerator[0]
    groups = lax.axis_size("group")
    count = lax.axis_size("shard")
    level_count = groups.bit_length() - 1
    rows, width = own_state.shape
    units = rows * count
    tiles = width // LANES
    first = max(1, tiles // 6)
    plan = {
        "groups": groups,
        "far": count // NEAR,
        "near": NEAR,
        "rows": rows,
        "first": first,
        "pieces": tiles - first,
        "splits": 2 if rows % 32 == 0 else 1,
        "tile": next(t for t in (1152, units) if units % t == 0 and t % (NEAR * rows) == 0),
        "offsets": tuple(1 << bit for bit in range(level_count)),
    }
    weight = jnp.broadcast_to(push_weight[0], (8, LANES))
    gradient, totals, peer_states, peer_grads = reduced(hidden[0], upstream[0], own_state, weight, plan)
    mixed_state, new_params, weight_next = updated(
        step_index, totals, own_state, gradient, peer_states, peer_grads, units * width
    )
    return (mixed_state[None], weight_next, new_params[None])


def solution(mesh):
    placed = (
        P(),
        P("group", "shard", None),
        P("group", "shard", None),
        P("group", "shard", None),
        P("group"),
    )
    return jax.shard_map(
        shards,
        mesh=mesh,
        in_specs=placed,
        out_specs=(P("group", "shard", None), P("group"), P("group", "shard", None)),
        check_vma=False,
    )
```

time: 274 us -> 253 us (0.923)
  matrix products: 15.1 us -> 0 us
  Pallas kernels: 236 us -> 250 us
  other arithmetic: 13.8 us -> 0 us
  between operations: 5.73 us -> 1.93 us
    dot_general x1 -> x0, matrix products: 15.1 us -> none  [shards(): lax.dot_general(hidden[0], upstream[0][:, :columns], (((0,), (0,)), ((),...]
    pallas_call x1 -> x2, Pallas kernels: 236 us -> 250 us  [the longest x1 240 us: reduced(): pl.pallas_call(functools.partial(kernel, plan), out_shape=[jax.ShapeDtype...]
    broadcast_in_dim x1 -> x0, other arithmetic: 8.7 us -> none  [shards(): return (mixed_state[None], weight_next, new_params[None])]
    convert_element_type x1 -> x0, other arithmetic: 4.27 us -> none  [shards(): own_state.astype(LINKED)]
where the time goes in v1:
time: 253 us; the launch traced here: 252 us
  Pallas kernels  250 us (99%)
    pallas_call x1, Pallas kernels, reduced(): pl.pallas_call(functools.partial(kernel, plan), out_shape=[jax.ShapeDtype...  240 us
    pallas_call x1, Pallas kernels, updated(): pl.pallas_call(functools.partial(update, levels, entry_count), out_shape=...  10.2 us

profile of v1, /device:TPU:0, one launch (start us, length us, event | category | flops | bytes accessed | tf_op | source)
XLA Modules:
  0.0 252.3 jit_solution(17823390434491028820)
XLA Ops:
  1.9 0.6 broadcast_in_dim.9.weight
  2.5 239.5 %shard_map.76 = (bf16[576,2304]{1,0:T(8,128)(2,1)}, f32[3,2,8,128]{3,2,1,0:T(8,128)}, bf16[2,576,2304]{2,1,0:T(8,128)(2,1)}, bf16[2,576,2304]{2,1,0:T(8,128)(2,1)}) custom-call(bf16[1024,4608]{1,0:T(8,128)(2,1)} %bitcast.9, bf16[1024,2304]{1,0:T(8,128)(2,1)} %bitcast.10, f32[576,2304]{1,0:T(8,128)} %bitcast.7, f32[8,128]{1,0:T(8,128)} %broadcast_in_dim.9.weight), custom_call_target="tpu_custom_call" | custom-call | tf_op jit(solution)/shard_map/pallas_call | solution.py:414
  242.1 10.2 %shard_map.77 = (f32[576,2304]{1,0:T(8,128)}, bf16[576,2304]{1,0:T(8,128)(2,1)}, f32[1]{0:T(128)}) custom-call(s32[1]{0:T(128)S(6)} %copy.8.step, f32[3,2,8,128]{3,2,1,0:T(8,128)} %get-tuple-element.10.totals, f32[576,2304]{1,0:T(8,128)} %bitcast.8, bf16[576,2304]{1,0:T(8,128)(2,1)} %get-tuple-element.11.grad, ...), custom_call_target="tpu_custom_call" | custom-call | tf_op jit(solution)/shard_map/pallas_call | solution.py:454

commit v2 on v1

--- a/solution.py
+++ b/solution.py
@@ -18,6 +18,12 @@
 AHEAD = 3
 RING = 4
 FLIGHT = 2
+EDGE = 1
+MIDDLE = 2
+START = 2
+LAG = 1
+DRAIN = 10
+UPDATE = 144
 
 
 def wide(x):
@@ -36,9 +42,9 @@
     first, pieces, splits, tile = (plan[k] for k in ("first", "pieces", "splits", "tile"))
     levels, count, half = len(offsets), far * near, rows // splits
     (units, cotangent, own, away, came, slots, first_own, first_slots, turn_own, turn_out, turn_in, cast, stage,
-     running, norms, fetch_sem, stage_sem, near_send, near_recv, up_send, up_recv, down_send, down_recv,
+     running, summed, weights, norms, fetch_sem, stage_sem, near_send, near_recv, up_send, up_recv, down_send, down_recv,
      first_up_send, first_up_recv, first_down_send, first_down_recv, turn_send, turn_recv, state_send, state_recv,
-     grad_send, grad_recv, norm_send, norm_recv) = refs
+     grad_send, grad_recv, norm_send, norm_recv, weight_send, weight_recv) = refs
 
     g, s = lax.axis_index("group"), lax.axis_index("shard")
     z, y = s // near, s % near
@@ -60,7 +66,7 @@
         )
 
     def part(h):
-        return pl.ds(h * half, half)
+        return pl.ds(h * half if isinstance(h, int) else pl.multiple_of(h * half, half), half)
 
     def columns(at, size=LANES):
         return pl.ds(pl.multiple_of(at * LANES, LANES), size)
@@ -95,6 +101,10 @@
 
     def state_copy(l):
         return remote(cast, peer_states.at[l], state_send.at[l], state_recv.at[l], ((g + offsets[l]) % groups, s))
+
+    def weight_copy(l):
+        to = weights.at[l + 1]
+        return remote(weight, to, weight_send.at[l], weight_recv.at[l], ((g + offsets[l]) % groups, s))
 
     def grad_copy(at, h, l):
         return remote(
@@ -182,14 +192,14 @@
     def term(c, h, b):
         return wide(own[c, b, part(h), :]) + wide(came[c, b, part(h), :])
 
-    def line_step(c, h, t):
+    def line_step(c, h, t, edge, middle):
         def fill(b, add):
             value = term(c, h, b)
             if add:
                 value = value + wide(slots[c, b, part(h), :])
             slots[c, b, part(h), :] = value.astype(LINKED)
 
-        line(t, True, True, fill, lambda t, b: up_copy(c, h, t, b), lambda t, b: down_copy(c, h, t, b))
+        line(t, edge, middle, fill, lambda t, b: up_copy(c, h, t, b), lambda t, b: down_copy(c, h, t, b))
 
     def first_step(j, t, edge, middle):
         def fill(b, add):
@@ -210,7 +220,7 @@
         total = square[0:8]
         for i in range(8, half, 8):
             total = total + square[i : i + 8]
-        running[0] = running[0] + total
+        running[...] = running[...] + total
         for l in range(levels):
             grad_copy(at, h, l).start()
 
@@ -254,8 +264,11 @@
     span = max(1, pieces - 3)
 
     def reached(c):
-        goal = far - 1 + lax.div((c + 1) * (steps - (far - 1)), span)
-        return jnp.where(c < 0, 0, jnp.minimum(steps, goal))
+        goal = START + lax.div((c + 1) * (steps - START), span)
+        return jnp.where(c < 0, START, jnp.minimum(steps, goal))
+
+    def crossed(c):
+        return jnp.where(c < LAG, 0, reached(c - LAG))
 
     def when(condition, body):
         pl.when(condition)(body)
@@ -265,18 +278,22 @@
     loop(0, chunks, lambda k: fetch_units(k).start())
     fetch_cotangent(1, lead[1], first + pieces).start()
     fetch_cotangent(2, 0, lead[0]).start()
-    running[0] = jnp.zeros((8, LANES), jnp.float32)
-    running[1] = weight[...]
+    running[...] = jnp.zeros((8, LANES), jnp.float32)
+    weights[0] = weight[...]
     fetch_cotangent(0, *lead).wait()
     compute(first - 1, [("first", 0), ("near", 0)], loading=True)
     pl.semaphore_wait(barrier, len(receivers))
-    for k in range(FLIGHT):
-        near_copy(k // splits, k % splits).start()
-    loop(0, far - 1, lambda t: first_step(0, t, True, False))
+    near_copy(0, 0).start()
+    first_step(0, 0, True, False)
     fetch_cotangent(1, lead[1], first + pieces).wait()
     fetch_cotangent(2, 0, lead[0]).wait()
     compute(first + 1, [("near", c) for c in range(1, AHEAD)])
+    for k in range(1, FLIGHT):
+        near_copy(k // splits, k % splits).start()
     compute(0, [("first", j) for j in range(first - 1, 0, -1)])
+
+    for q in range(1, START):
+        first_step(q // (far - 1), q % (far - 1), True, False)
 
     def stage_copy(i):
         return pltpu.make_async_copy(
@@ -293,65 +310,13 @@
     loop(0, rows // chunk_rows, cast_rows)
     for l in range(levels):
         state_copy(l).start()
+        weight_copy(l).start()
 
     def prepare(c):
         for h in range(splits):
             when(c >= RING, lambda: near_copy(c - RING, h).wait_send())
         compute(first + c, [("near", c)])
 
-    def tick(c):
-        for h in range(splits):
-            done = c - (far - 1)
-            when((done >= 0) & (done < pieces), lambda: finish(done, h))
-
-            def older(i):
-                t = far - 2 - i
-                when((c - t >= 0) & (c - t < pieces), lambda: line_step(c - t, h, t))
-
-            loop(0, far - 2, older)
-
-            @pl.when(c < pieces)
-            def _():
-                near_copy(c, h).wait_recv()
-                later = c + (h + FLIGHT) // splits
-                when(later < pieces, lambda: near_copy(later, (h + FLIGHT) % splits).start())
-                line_step(c, h, 0)
-
-            if h == 0:
-                when(c + AHEAD < pieces, lambda: prepare(c + AHEAD))
-        loop(lax.div(reached(c - 3), far - 1), lax.div(reached(c - 2), far - 1), finish_turn)
-        loop(lax.div(reached(c - 2), far - 1), lax.div(reached(c - 1), far - 1), finish_first)
-
-        def first_at(q):
-            j, t = lax.div(q, far - 1), lax.rem(q, far - 1)
-            when(j > 0, lambda: first_step(j, t, True, False))
-            first_step(j, t, False, True)
-
-        loop(reached(c - 1), reached(c), first_at)
-
-    loop(0, pieces + far - 1, tick)
-
-    def norm_copy(l, s_from, e):
-        d = 0 if l == 0 else offsets[l - 1]
-        at = norms.at[l, s_from]
-        return remote(running, at, norm_send.at[l, e], norm_recv.at[l, e], ((g + d) % groups, (s + e) % count))
-
-    messages = [(l, e) for l in range(levels + 1) for e in range(count) if l or e]
-    for l, e in messages:
-        norm_copy(l, s, e).start()
-    norms[0, s] = running[...]
-    for l, e in messages:
-        norm_copy(l, (s + count - e) % count, e).wait_recv()
-    for l in range(levels + 1):
-        total = norms[l, 0, 0]
-        for d in range(1, count):
-            total = total + norms[l, d, 0]
-        totals[l, 0] = total
-        totals[l, 1] = norms[l, 0, 1]
-
-    for l, e in messages:
-        norm_copy(l, s, e).wait_send()
-
     def drain_line(t, up, down):
         @pl.when((z <= t) & (z < far - 1))
         def _():
@@ -361,11 +326,69 @@
         def _():
             down(t, t - (far - 1) + z).wait_send()
 
-    def drain(c):
-        for h in range(splits):
-            when(c >= pieces - RING, lambda: near_copy(c, h).wait_send())
-            loop(0, far - 1, lambda t: drain_line(
-                t, lambda t, b: up_copy(c, h, t, b), lambda t, b: down_copy(c, h, t, b)))
+    def drain(c, h):
+        when(c >= pieces - RING, lambda: near_copy(c, h).wait_send())
+        loop(0, far - 1, lambda t: drain_line(
+            t, lambda t, b: up_copy(c, h, t, b), lambda t, b: down_copy(c, h, t, b)))
+
+    total_pieces = pieces * splits
+
+    def piece(k, body):
+        when((k >= 0) & (k < total_pieces), lambda: body(lax.div(k, splits), lax.rem(k, splits)))
+
+    def tick(k):
+        piece(k - MIDDLE * (far - 1), finish)
+
+        def middle_step(i):
+            t = far - 2 - i
+            piece(k - MIDDLE * t, lambda c, h: line_step(c, h, t, False, True))
+
+        def edge_step(i):
+            t = far - 2 - i
+            piece(k - EDGE * t, lambda c, h: line_step(c, h, t, True, False))
+
+        def newest(c, h):
+            near_copy(c, h).wait_recv()
+            piece(k + FLIGHT, lambda c, h: near_copy(c, h).start())
+            line_step(c, h, 0, True, False)
+
+        loop(0, far - 2, middle_step)
+        loop(0, far - 2, edge_step)
+        piece(k, newest)
+        c = lax.div(k, splits)
+
+        @pl.when(lax.rem(k, splits) == 0)
+        def _():
+            when(c + AHEAD < pieces, lambda: prepare(c + AHEAD))
+
+        @pl.when(lax.rem(k, splits) == splits - 1)
+        def _():
+            loop(lax.div(crossed(c - 2), far - 1), lax.div(crossed(c - 1), far - 1), finish_turn)
+            loop(lax.div(crossed(c - 1), far - 1), lax.div(crossed(c), far - 1), finish_first)
+
+            def first_edge(q):
+                first_step(lax.div(q, far - 1), lax.rem(q, far - 1), True, False)
+
+            def first_middle(q):
+                first_step(lax.div(q, far - 1), lax.rem(q, far - 1), False, True)
+
+            loop(reached(c - 1), reached(c), first_edge)
+            loop(crossed(c), crossed(c + 1), first_middle)
+
+        piece(k - DRAIN, drain)
+
+    loop(0, total_pieces + MIDDLE * (far - 1), tick)
+
+    def norm_copy(l, s_from, e):
+        d = 0 if l == 0 else offsets[l - 1]
+        at = norms.at[l, s_from]
+        return remote(summed, at, norm_send.at[l, e], norm_recv.at[l, e], ((g + d) % groups, (s + e) % count))
+
+    summed[...] = jnp.sum(running[...], axis=0, keepdims=True)
+    messages = [(l, e) for l in range(levels + 1) for e in range(count) if l or e]
+    for l, e in messages:
+        norm_copy(l, s, e).start()
+    norms[0, s] = summed[...]
 
     def drain_first(j):
         loop(0, far - 1, lambda t: drain_line(
@@ -376,11 +399,22 @@
             for l in range(levels):
                 grad_copy(at, h, l).wait()
 
-    loop(0, pieces, drain)
-    loop(0, first, drain_first)
-    loop(0, first + pieces, drain_grads)
     for l in range(levels):
         state_copy(l).wait()
+        weight_copy(l).wait()
+    loop(0, first, drain_first)
+    loop(max(0, total_pieces + MIDDLE * (far - 1) - DRAIN), total_pieces, lambda k: piece(k, drain))
+    loop(0, first + pieces, drain_grads)
+    for l, e in messages:
+        norm_copy(l, (s + count - e) % count, e).wait_recv()
+    for l in range(levels + 1):
+        total = norms[l, 0]
+        for d in range(1, count):
+            total = total + norms[l, d]
+        totals[l, 0] = total
+        totals[l, 1] = weights[l]
+    for l, e in messages:
+        norm_copy(l, s, e).wait_send()
 
 
 def reduced(hidden, upstream, state, weight, plan):
@@ -402,20 +436,22 @@
         pltpu.VMEM((first, rows, LANES), LINKED),
         pltpu.VMEM((rows, width), LINKED),
         pltpu.VMEM((2, step_of_rows(rows), width), single),
-        pltpu.VMEM((2, 8, LANES), single),
-        pltpu.VMEM((levels + 1, count, 2, 8, LANES), single),
+        pltpu.VMEM((8, LANES), single),
+        pltpu.VMEM((1, LANES), single),
+        pltpu.VMEM((levels + 1, 1, LANES), single),
+        pltpu.VMEM((levels + 1, count, 1, LANES), single),
         dma((far * near * rows // plan["tile"] + 3,)),
         dma((2,)),
     ]
     scratch += [dma((pieces, splits))] * 2 + [dma((pieces, splits, far - 1))] * 4 + [dma((first, far - 1))] * 4
     scratch += [dma((first,))] * 2 + [dma((levels,))] * 2 + [dma((first + pieces, splits, levels))] * 2
-    scratch += [dma((levels + 1, count))] * 2
+    scratch += [dma((levels + 1, count))] * 2 + [dma((levels,))] * 2
     peers = jax.ShapeDtypeStruct((levels, rows, width), LINKED)
     return pl.pallas_call(
         functools.partial(kernel, plan),
         out_shape=[
             jax.ShapeDtypeStruct((rows, width), LINKED),
-            jax.ShapeDtypeStruct((levels + 1, 2, 8, LANES), single),
+            jax.ShapeDtypeStruct((levels + 1, 2, 1, LANES), single),
             peers,
             peers,
         ],
@@ -428,27 +464,32 @@
     )(hidden, upstream, state, weight)
 
 
-def update(levels, entry_count, step, totals, state, grad, peer_state, peer_grad, mixed_out, params_out, weight_out):
-    bit = lax.rem(step[0], levels)
-    rate = learning_rate / jnp.sqrt(1.0 + jnp.full((8, LANES), step[0], jnp.int32).astype(jnp.float32) / decay_steps)
-
-    def factor(l):
-        squares = jnp.sum(totals[l, 0], keepdims=True)
-        return (rate * jnp.minimum(1.0, clip_ceiling / jnp.sqrt(squares / entry_count + epsilon)))[0:1, 0:1]
-
-    mine, other = factor(0), factor(1 + bit)
-    weight_next = 0.5 * (totals[0, 1] + totals[1 + bit, 1])
-    weight_out[0] = jnp.max(weight_next)
-    pushed = state[...] - mine * wide(grad[...])
-    came = wide(peer_state[0]) - other * wide(peer_grad[0])
-    mixed = 0.5 * (pushed + came)
+def update(levels, entry_count, step, totals, state, grad, peer_state, peer_grad, mixed_out, params_out, weight_out, held):
+    @pl.when(pl.program_id(0) == 0)
+    def _():
+        bit = lax.rem(step[0], levels)
+        when = jnp.full((1, LANES), step[0], jnp.int32).astype(jnp.float32)
+        rate = learning_rate / jnp.sqrt(1.0 + when / decay_steps)
+
+        def factor(l):
+            squares = jnp.sum(totals[l, 0], keepdims=True)
+            return rate * jnp.minimum(1.0, clip_ceiling / jnp.sqrt(squares / entry_count + epsilon))
+
+        weight_next = 0.5 * (totals[0, 1] + totals[1 + bit, 1])
+        weight_out[0] = jnp.max(weight_next)
+        held[0] = 0.5 * factor(0)
+        held[1] = 0.5 * factor(1 + bit)
+        held[2] = 1.0 / weight_next
+
+    mine, other, scale = (held[i, 0:1, 0:1] for i in range(3))
+    mixed = 0.5 * (state[...] + wide(peer_state[0])) - (mine * wide(grad[...]) + other * wide(peer_grad[0]))
     mixed_out[...] = mixed
-    params_out[...] = (mixed * (1.0 / weight_next)[0:1, 0:1]).astype(jnp.bfloat16)
+    params_out[...] = (mixed * scale).astype(jnp.bfloat16)
 
 
 def updated(step_index, totals, state, grad, peer_states, peer_grads, entry_count):
     levels, (rows, width) = peer_states.shape[0], state.shape
-    step = step_of_rows(rows)
+    step = next(t for t in (UPDATE, step_of_rows(rows)) if rows % t == 0)
     here = pl.BlockSpec((step, width), lambda i, at: (i, 0))
     chosen = pl.BlockSpec((1, step, width), lambda i, at: (lax.rem(at[0], levels), i, 0))
     return pl.pallas_call(
@@ -463,6 +504,7 @@
             grid=(rows // step,),
             in_specs=[pl.BlockSpec(totals.shape, lambda i, at: (0, 0, 0, 0)), here, here, chosen, chosen],
             out_specs=[here, here, pl.BlockSpec(memory_space=pltpu.SMEM)],
+            scratch_shapes=[pltpu.VMEM((3, 1, LANES), jnp.float32)],
         ),
     )(step_index, totals, state, grad, peer_states, peer_grads)
 
@@ -487,7 +529,7 @@
         "tile": next(t for t in (1152, units) if units % t == 0 and t % (NEAR * rows) == 0),
         "offsets": tuple(1 << bit for bit in range(level_count)),
     }
-    weight = jnp.broadcast_to(push_weight[0], (8, LANES))
+    weight = jnp.broadcast_to(push_weight[0], (1, LANES))
     gradient, totals, peer_states, peer_grads = reduced(hidden[0], upstream[0], own_state, weight, plan)
     mixed_state, new_params, weight_next = updated(
         step_index, totals, own_state, gradient, peer_states, peer_grads, units * width

time: 253 us -> 247 us (0.976)
  Pallas kernels: 250 us -> 244 us
    pallas_call x1, Pallas kernels: 240 us -> 235 us  [reduced(): pl.pallas_call(functools.partial(kernel, plan), out_shape=[jax.ShapeDtype...]
where the time goes in v2:
time: 247 us
  Pallas kernels  244 us (99%)
    pallas_call x1, Pallas kernels, reduced(): pl.pallas_call(functools.partial(kernel, plan), out_shape=[jax.ShapeDtype...  235 us
    pallas_call x1, Pallas kernels, updated(): pl.pallas_call(functools.partial(update, levels, entry_count), out_shape=...  9.17 us

profile of v2, /device:TPU:0, one launch (start us, length us, event | category | flops | bytes accessed | tf_op | source)
XLA Modules:
  0.0 246.9 jit_solution(3132819235998262679)
XLA Ops:
  1.9 0.5 broadcast_in_dim.9.weight
  2.4 235.2 %shard_map.76 = (bf16[576,2304]{1,0:T(8,128)(2,1)}, f32[3,2,1,128]{3,2,1,0:T(1,128)}, bf16[2,576,2304]{2,1,0:T(8,128)(2,1)}, bf16[2,576,2304]{2,1,0:T(8,128)(2,1)}) custom-call(bf16[1024,4608]{1,0:T(8,128)(2,1)} %bitcast.9, bf16[1024,2304]{1,0:T(8,128)(2,1)} %bitcast.10, f32[576,2304]{1,0:T(8,128)} %bitcast.7, f32[1,128]{1,0:T(1,128)} %broadcast_in_dim.9.weight), custom_call_target="tpu_custom_call" | custom-call | tf_op jit(solution)/shard_map/pallas_call | solution.py:450
  237.7 9.2 %shard_map.77 = (f32[576,2304]{1,0:T(8,128)}, bf16[576,2304]{1,0:T(8,128)(2,1)}, f32[1]{0:T(128)}) custom-call(s32[1]{0:T(128)S(6)} %copy.8.step, f32[3,2,1,128]{3,2,1,0:T(1,128)} %get-tuple-element.10.totals, f32[576,2304]{1,0:T(8,128)} %bitcast.8, bf16[576,2304]{1,0:T(8,128)(2,1)} %get-tuple-element.11.grad, ...), custom_call_target="tpu_custom_call" | custom-call | tf_op jit(solution)/shard_map/pallas_call | solution.py:495

commit v3 on v2

--- a/solution.py
+++ b/solution.py
@@ -44,7 +44,7 @@
     (units, cotangent, own, away, came, slots, first_own, first_slots, turn_own, turn_out, turn_in, cast, stage,
      running, summed, weights, norms, fetch_sem, stage_sem, near_send, near_recv, up_send, up_recv, down_send, down_recv,
      first_up_send, first_up_recv, first_down_send, first_down_recv, turn_send, turn_recv, state_send, state_recv,
-     grad_send, grad_recv, norm_send, norm_recv, weight_send, weight_recv) = refs
+     grad_send, grad_recv, norm_send, norm_recv, weight_send, weight_recv, lead_send, lead_recv) = refs
 
     g, s = lax.axis_index("group"), lax.axis_index("shard")
     z, y = s // near, s % near
@@ -75,6 +75,10 @@
         return remote(
             away.at[c % RING, :, part(h)], came.at[c, :, part(h)], near_send.at[c, h], near_recv.at[c, h], near_peer
         )
+
+    def lead_copy(k):
+        to = pl.ds(k * blocks, blocks)
+        return remote(away.at[0, to], came.at[0, to], lead_send.at[k], lead_recv.at[k], near_peer)
 
     def up_copy(c, h, t, b):
         at = slots.at[c, b, part(h)]
@@ -139,11 +143,11 @@
         at = pl.ds(low * LANES, (high - low) * LANES)
         return pltpu.make_async_copy(upstream.at[:, at], cotangent.at[:, at], fetch_sem.at[chunks + i])
 
-    def compute(at, places, loading=False):
+    def compute(at, places, after=None):
         size = len(places) * LANES
 
         def once(k):
-            if loading:
+            if after:
                 fetch_units(k).wait()
             product = lax.dot_general(
                 units[:, pl.ds(pl.multiple_of(k * tile, tile), tile)],
@@ -160,6 +164,9 @@
                     own[index, to] = jnp.where(y == 0, piece[:, 0], piece[:, 1]).astype(LINKED)
                     away[index % RING, to] = jnp.where(y == 0, piece[:, 1], piece[:, 0]).astype(LINKED)
 
+            if after:
+                after(k)
+
         loop(0, chunks, once)
 
     def line(t, edge, middle, fill, up, down):
@@ -281,15 +288,17 @@
     running[...] = jnp.zeros((8, LANES), jnp.float32)
     weights[0] = weight[...]
     fetch_cotangent(0, *lead).wait()
-    compute(first - 1, [("first", 0), ("near", 0)], loading=True)
-    pl.semaphore_wait(barrier, len(receivers))
-    near_copy(0, 0).start()
+
+    def after(k):
+        when(k == 0, lambda: pl.semaphore_wait(barrier, len(receivers)))
+        lead_copy(k).start()
+
+    compute(first - 1, [("first", 0), ("near", 0)], after)
     first_step(0, 0, True, False)
     fetch_cotangent(1, lead[1], first + pieces).wait()
     fetch_cotangent(2, 0, lead[0]).wait()
     compute(first + 1, [("near", c) for c in range(1, AHEAD)])
-    for k in range(1, FLIGHT):
-        near_copy(k // splits, k % splits).start()
+    near_copy(1, 0).start()
     compute(0, [("first", j) for j in range(first - 1, 0, -1)])
 
     for q in range(1, START):
@@ -313,8 +322,9 @@
         weight_copy(l).start()
 
     def prepare(c):
+        when(c == RING, lambda: loop(0, chunks, lambda k: lead_copy(k).wait_send()))
         for h in range(splits):
-            when(c >= RING, lambda: near_copy(c - RING, h).wait_send())
+            when(c > RING, lambda: near_copy(c - RING, h).wait_send())
         compute(first + c, [("near", c)])
 
     def drain_line(t, up, down):
@@ -348,8 +358,9 @@
             piece(k - EDGE * t, lambda c, h: line_step(c, h, t, True, False))
 
         def newest(c, h):
-            near_copy(c, h).wait_recv()
-            piece(k + FLIGHT, lambda c, h: near_copy(c, h).start())
+            when(c == 0, lambda: when(h == 0, lambda: loop(0, chunks, lambda k: lead_copy(k).wait_recv())))
+            when(c > 0, lambda: near_copy(c, h).wait_recv())
+            when(k + FLIGHT > splits, lambda: piece(k + FLIGHT, lambda c, h: near_copy(c, h).start()))
             line_step(c, h, 0, True, False)
 
         loop(0, far - 2, middle_step)
@@ -446,6 +457,7 @@
     scratch += [dma((pieces, splits))] * 2 + [dma((pieces, splits, far - 1))] * 4 + [dma((first, far - 1))] * 4
     scratch += [dma((first,))] * 2 + [dma((levels,))] * 2 + [dma((first + pieces, splits, levels))] * 2
     scratch += [dma((levels + 1, count))] * 2 + [dma((levels,))] * 2
+    scratch += [dma((far * near * rows // plan["tile"],))] * 2
     peers = jax.ShapeDtypeStruct((levels, rows, width), LINKED)
     return pl.pallas_call(
         functools.partial(kernel, plan),

time: 247 us -> 246 us (level)
  no operation moved by 1% of the time
where the time goes in v3:
time: 246 us; the launch traced here: 245 us
  Pallas kernels  243 us (99%)
    pallas_call x1, Pallas kernels, reduced(): pl.pallas_call(functools.partial(kernel, plan), out_shape=[jax.ShapeDtype...  234 us
    pallas_call x1, Pallas kernels, updated(): pl.pallas_call(functools.partial(update, levels, entry_count), out_shape=...  9.17 us

profile of v3, /device:TPU:0, one launch (start us, length us, event | category | flops | bytes accessed | tf_op | source)
XLA Modules:
  0.0 245.1 jit_solution(1207777439000947412)
XLA Ops:
  1.9 0.5 broadcast_in_dim.9.weight
  2.4 233.5 %shard_map.76 = (bf16[576,2304]{1,0:T(8,128)(2,1)}, f32[3,2,1,128]{3,2,1,0:T(1,128)}, bf16[2,576,2304]{2,1,0:T(8,128)(2,1)}, bf16[2,576,2304]{2,1,0:T(8,128)(2,1)}) custom-call(bf16[1024,4608]{1,0:T(8,128)(2,1)} %bitcast.9, bf16[1024,2304]{1,0:T(8,128)(2,1)} %bitcast.10, f32[576,2304]{1,0:T(8,128)} %bitcast.7, f32[1,128]{1,0:T(1,128)} %broadcast_in_dim.9.weight), custom_call_target="tpu_custom_call" | custom-call | tf_op jit(solution)/shard_map/pallas_call | solution.py:462
  236.0 9.2 %shard_map.77 = (f32[576,2304]{1,0:T(8,128)}, bf16[576,2304]{1,0:T(8,128)(2,1)}, f32[1]{0:T(128)}) custom-call(s32[1]{0:T(128)S(6)} %copy.8.step, f32[3,2,1,128]{3,2,1,0:T(1,128)} %get-tuple-element.10.totals, f32[576,2304]{1,0:T(8,128)} %bitcast.8, bf16[576,2304]{1,0:T(8,128)(2,1)} %get-tuple-element.11.grad, ...), custom_call_target="tpu_custom_call" | custom-call | tf_op jit(solution)/shard_map/pallas_call | solution.py:507
